TPU v7x, 32 devices: a whole 2x2x4 slice. The times are simulated.
32 devices in a mesh: region: 2 (over x), leaf: 16 (over z, y, core).
Axes of the slice: x: 2, y: 2, z: 4, core: 2. Of those that a mesh axis runs over, the one named last changes fastest.
Arguments:
- whiten: bfloat16 [32, 1024, 1024], P(('region', 'leaf')), as said below
- leaf_root: bfloat16 [32, 1024, 512], P(('region', 'leaf')), may hold values from -6 to 6
- leaf_region: bfloat16 [32, 1024, 512], P(('region', 'leaf')), may hold values from -6 to 6
- root_factor: bfloat16 [512, 512], P('region'), may hold values from -0.25 to 0.25
- root_adjoint: bfloat16 [512, 512], P('region'), may hold values from -0.25 to 0.25
- region_factor: bfloat16 [2, 512, 512], P('region', 'leaf'), may hold values from -0.25 to 0.25
- region_adjoint: bfloat16 [2, 512, 512], P('region', 'leaf'), may hold values from -0.25 to 0.25
Outputs:
- grad_root_basis: bfloat16 [32, 1024, 512], P(('region', 'leaf'))
- grad_region_basis: bfloat16 [32, 1024, 512], P(('region', 'leaf'))
- grad_root_factor: float32 [512, 512], P('leaf')
- grad_region_factor: float32 [2, 512, 512], P('region', 'leaf')
Inputs may be any that keep to these rules, and one draw needn't show every extreme that they name: `whiten`: each whitening matrix is lower triangular with a positive diagonal.
All inputs are finite; a program needn't handle non-finite values.
Results may differ from a plain program's by a relative error of at most 0.018.
Values may be sent and summed in bfloat16 or wider, within the bound.
A program may use at most 64 MiB of HBM per device.

v0:
```python
import functools
import math

import jax
import jax.numpy as jnp
from jax import lax
from jax.experimental import pallas as pl
from jax.experimental.pallas import tpu as pltpu
from jax.sharding import PartitionSpec as P

MESH = pl.DeviceIdType.MESH
F32, BF16 = jnp.float32, jnp.bfloat16


def split_leaf(leaves):
    chips = leaves // 2
    fast = max(d for d in range(1, math.isqrt(chips) + 1) if chips % d == 0)
    return chips // fast, fast


def offset(value, step, count):
    if count & (count - 1):
        return lax.rem(value + step, count), lax.rem(value + count - step, count)
    bit = 1
    pair = value
    while bit < count:
        if step & bit:
            pair = pair + bit - 2 * bit * lax.rem(value // bit, 2)
        bit *= 2
    return pair, pair


def dot(left, right):
    return jnp.dot(left, right, preferred_element_type=F32)


def kernel(
    nr, nl,
    w_in, lr_in, lg_in, rf_in, ra_in, gf_in, ga_in,
    gr_out, gg_out, fr_out, fg_out,
    w, l, a, b, rt, rg, g, grad, cb, rc, ys, ry, zs, rz, rx,
    ld, st, gz_s, gz_r, gy_s, gy_r, gc_s, gc_r, gx_s, gx_r, gp_s, gp_r,
    cs_s, cs_r, ys_s, ys_r, zs_s, zs_r, xs_s, xs_r,
):
    Z, Y = split_leaf(nl)
    obs, K = l.shape[1], l.shape[2]
    rows, half = K // nl, K // nr
    T = min(256, K)
    nb = obs // T
    r, leaf = lax.axis_index("region"), lax.axis_index("leaf")
    c, y, z = lax.rem(leaf, 2), lax.rem(leaf // 2, Y), leaf // (2 * Y)
    oc = 1 - c

    def at(zz, yy, cc):
        return (zz * Y + yy) * 2 + cc

    def zp(k):
        return offset(z, k, Z)[0]

    def zm(k):
        return offset(z, k, Z)[1]

    def yp(k):
        return offset(y, k, Y)[0]

    def ym(k):
        return offset(y, k, Y)[1]

    def rp(k):
        return lax.rem(r + k, nr)

    def rm(k):
        return lax.rem(r + nr - k, nr)

    def span(index, size):
        return pl.ds(pl.multiple_of(index * size, size), size)

    mine = span(leaf, rows)
    own = span(r, half)
    loads = [
        pltpu.make_async_copy(gf_in.at[0], rg.at[0, mine], ld.at[0]),
        pltpu.make_async_copy(ga_in.at[0], rg.at[1, mine], ld.at[1]),
        pltpu.make_async_copy(rf_in, rt.at[0, own], ld.at[2]),
        pltpu.make_async_copy(ra_in, rt.at[1, own], ld.at[3]),
        pltpu.make_async_copy(lr_in.at[0], l.at[0], ld.at[4]),
        pltpu.make_async_copy(w_in.at[0], w, ld.at[5]),
        pltpu.make_async_copy(lg_in.at[0], l.at[1], ld.at[6]),
    ]
    for load in loads:
        load.start()

    barrier = pltpu.get_barrier_semaphore()
    peers = [{"leaf": at(zp(k), y, c)} for k in range(1, Z)]
    peers += [{"leaf": at(z, yp(k), c)} for k in range(1, Y)]
    peers += [{"leaf": at(z, y, oc)}]
    peers += [{"region": rp(k)} for k in range(1, nr)]
    for peer in peers:
        pl.semaphore_signal(barrier, inc=1, device_id=peer, device_id_type=MESH)
    for load in loads[:4]:
        load.wait()
    pl.semaphore_wait(barrier, len(peers))

    sends = []

    def remote(src, dst, ssem, rsem, peer):
        return pltpu.make_async_remote_copy(
            src_ref=src, dst_ref=dst, send_sem=ssem, recv_sem=rsem,
            device_id=peer, device_id_type=MESH,
        )

    def send(src, dst, ssem, rsem, peer):
        copy = remote(src, dst, ssem, rsem, peer)
        copy.start()
        sends.append(copy)

    def arrive(ref, ssem, rsem, peer):
        remote(ref, ref, ssem, rsem, peer).wait_recv()

    other = {"leaf": at(z, y, oc)}

    def block(kz, ky, cc):
        return rg.at[:, span(at(zm(kz), ym(ky), cc), rows)]

    def gather_y(kz):
        for ky in range(1, Y):
            i = (ky - 1) * Z + kz
            send(block(kz, 0, c), block(kz, 0, c), gy_s.at[i], gy_r.at[i], {"leaf": at(z, yp(ky), c)})

    def gather_core(kz, ky):
        i = ky * Z + kz
        send(block(kz, ky, c), block(kz, ky, c), gc_s.at[i], gc_r.at[i], other)

    def z_forward(kz):
        arrive(block(kz, 0, c), gz_s.at[kz - 1], gz_r.at[kz - 1], other)
        gather_y(kz)
        gather_core(kz, 0)

    def y_forward(kz, ky):
        i = (ky - 1) * Z + kz
        arrive(block(kz, ky, c), gy_s.at[i], gy_r.at[i], other)
        gather_core(kz, ky)

    for k in range(1, Z):
        send(block(0, 0, c), block(0, 0, c), gz_s.at[k - 1], gz_r.at[k - 1], {"leaf": at(zp(k), y, c)})
    gather_y(0)
    for k in range(1, nr):
        send(rt.at[c, own], rt.at[c, own], gx_s.at[k - 1], gx_r.at[k - 1], {"region": rp(k)})
    gather_core(0, 0)

    scale = 1.0 / obs

    def local_a(p):
        for n in range(K // T):
            cols = pl.ds(n * T, T)
            for i in range(nb):
                a[p, pl.ds(i * T, T), cols] = dot(
                    w[pl.ds(i * T, T), pl.ds(0, (i + 1) * T)], l[p, pl.ds(0, (i + 1) * T), cols]
                ).astype(BF16)

    def local_c(p):
        per = T // (2 * Y * rows) if T >= 2 * Y * rows else 0
        step = T if per else 2 * Y * rows
        per = step // (2 * Y * rows)
        for i in range(K // step):
            left = a[p, :, pl.ds(i * step, step)].T
            part = (dot(left, a[p]) * scale).astype(BF16)
            cb[p, pl.ds(i * per, per)] = part.reshape(per, Y, 2, rows, K)
        send(cb.at[p, :, :, oc], rc.at[p], cs_s.at[p], cs_r.at[p], other)

    def local_b(i):
        left = w[pl.ds(i * T, obs - i * T), pl.ds(i * T, T)].T
        for p in range(2):
            b[p, pl.ds(i * T, T), :] = dot(left, a[p, pl.ds(i * T, obs - i * T), :]).astype(BF16)

    far = range(Z - 1, -1, -1)

    def reduce_y(p):
        arrive(rc.at[p], cs_s.at[p], cs_r.at[p], other)
        for kz in far:
            zz = zp(kz)
            for k in range(1, Y):
                yy = yp(k)
                ys[p, k - 1, kz] = (cb[p, zz, yy, c].astype(F32) + rc[p, zz, yy].astype(F32)).astype(BF16)
                i = (p * Y + k) * Z + kz
                send(ys.at[p, k - 1, kz], ry.at[p, k - 1, kz], ys_s.at[i], ys_r.at[i], {"leaf": at(z, yy, c)})

    def chip_sum(p, kz):
        zz = zp(kz)
        total = cb[p, zz, y, c].astype(F32) + rc[p, zz, y].astype(F32)
        for k in range(1, Y):
            i = (p * Y + k) * Z + kz
            arrive(ry.at[p, k - 1, kz], ys_s.at[i], ys_r.at[i], other)
            total += ry[p, k - 1, kz].astype(F32)
        return total

    def reduce_z(p):
        for k in far[:-1]:
            zs[p, k - 1] = chip_sum(p, k).astype(BF16)
            i = p * Z + k
            send(zs.at[p, k - 1], rz.at[p, k - 1], zs_s.at[i], zs_r.at[i], {"leaf": at(zp(k), y, c)})

    def finish_z(p):
        total = chip_sum(p, 0)
        for k in range(1, Z):
            i = p * Z + k
            arrive(rz.at[p, k - 1], zs_s.at[i], zs_r.at[i], other)
            total += rz[p, k - 1].astype(F32)
        return total

    def make_g(p, held):
        factor, adjoint = held[0], held[1]
        both = dot(factor, adjoint) + lax.dot_general(
            factor, adjoint, (((1,), (1,)), ((), ())), preferred_element_type=F32
        )
        g[p] = both.astype(BF16)

    def make_grad(p, out):
        for i in range(nb):
            part = pl.ds(i * T, T)
            grad[p, part, :] = dot(b[p, part, :], g[p]).astype(BF16)
        copy = pltpu.make_async_copy(grad.at[p], out.at[0], st.at[p])
        copy.start()
        return copy

    loads[4].wait()
    loads[5].wait()
    local_a(0)
    local_c(0)
    if Z > 1:
        z_forward(1)
    loads[6].wait()
    local_a(1)
    local_c(1)
    if Z > 2:
        z_forward(2)
    local_b(0)
    reduce_y(0)
    for k in range(3, Z):
        z_forward(k)
    reduce_y(1)
    for i in range(1, nb):
        local_b(i)
    for ky in range(1, Y):
        y_forward(0, ky)
    reduce_z(0)
    for k in range(1, nr):
        theirs = rt.at[c, span(rm(k), half)]
        arrive(theirs, gx_s.at[k - 1], gx_r.at[k - 1], other)
        send(theirs, theirs, gp_s.at[k - 1], gp_r.at[k - 1], other)
    for ky in range(1, Y):
        for k in range(1, Z):
            y_forward(k, ky)
    reduce_z(1)
    for k in range(1, nr):
        arrive(rt.at[oc, span(rm(k), half)], gp_s.at[k - 1], gp_r.at[k - 1], other)
    make_g(0, rt)
    rx[r] = finish_z(0).astype(BF16)
    for k in range(1, nr):
        send(rx.at[r], rx.at[r], xs_s.at[k - 1], xs_r.at[k - 1], {"region": rp(k)})
    stores = [make_grad(0, gr_out)]
    for ky in range(Y):
        for kz in range(Z):
            i = ky * Z + kz
            arrive(block(kz, ky, oc), gc_s.at[i], gc_r.at[i], other)
    make_g(1, rg)
    stores.append(make_grad(1, gg_out))
    fg_out[0] = dot(finish_z(1).astype(BF16), g[1])
    for k in range(1, nr):
        arrive(rx.at[rm(k)], xs_s.at[k - 1], xs_r.at[k - 1], other)
    total = rx[0].astype(F32)
    for k in range(1, nr):
        total += rx[k].astype(F32)
    fr_out[...] = dot(total.astype(BF16), g[0])
    for copy in stores:
        copy.wait()
    for copy in sends:
        copy.wait_send()


def store(*refs):
    source, target, held = refs[:4], refs[4:8], refs[8:12]
    load_sem, store_sem = refs[12:]
    pieces = []
    for n in range(4):
        extent = source[n].shape[-2]
        size = min(extent, 256)
        for row in range(0, extent, size):
            where = (pl.ds(row, size),) if len(source[n].shape) == 2 else (0, pl.ds(row, size))
            pieces.append((source[n].at[where], held[n].at[where], target[n].at[where]))
    loads = [pltpu.make_async_copy(p[0], p[1], load_sem.at[i]) for i, p in enumerate(pieces)]
    stores = [pltpu.make_async_copy(p[1], p[2], store_sem.at[i]) for i, p in enumerate(pieces)]
    for load in loads:
        load.start()
    for load, save in zip(loads, stores):
        load.wait()
        save.start()
    for save in stores:
        save.wait()


def solution(mesh):
    nr, nl = mesh.shape["region"], mesh.shape["leaf"]
    Z, Y = split_leaf(nl)

    def on_device(whiten, leaf_root, leaf_region, root_factor, root_adjoint, region_factor, region_adjoint):
        obs, K = leaf_root.shape[1], leaf_root.shape[2]
        rows = K // nl
        dma = lambda n: pltpu.SemaphoreType.DMA((max(n, 1),))
        held = pl.pallas_call(
            functools.partial(kernel, nr, nl),
            out_shape=(
                jax.ShapeDtypeStruct(leaf_root.shape, BF16),
                jax.ShapeDtypeStruct(leaf_region.shape, BF16),
                jax.ShapeDtypeStruct((rows, K), F32),
                jax.ShapeDtypeStruct((1, rows, K), F32),
            ),
            in_specs=[pl.BlockSpec(memory_space=pltpu.HBM)] * 7,
            out_specs=(pl.BlockSpec(memory_space=pltpu.HBM),) * 2 + (pl.BlockSpec(memory_space=pltpu.VMEM),) * 2,
            scratch_shapes=[
                pltpu.VMEM((obs, obs), BF16),
                pltpu.VMEM((2, obs, K), BF16),
                pltpu.VMEM((2, obs, K), BF16),
                pltpu.VMEM((2, obs, K), BF16),
                pltpu.VMEM((2, K, K), BF16),
                pltpu.VMEM((2, K, K), BF16),
                pltpu.VMEM((2, K, K), BF16),
                pltpu.VMEM((2, obs, K), BF16),
                pltpu.VMEM((2, Z, Y, 2, rows, K), BF16),
                pltpu.VMEM((2, Z, Y, rows, K), BF16),
                pltpu.VMEM((2, max(Y - 1, 1), Z, rows, K), BF16),
                pltpu.VMEM((2, max(Y - 1, 1), Z, rows, K), BF16),
                pltpu.VMEM((2, max(Z - 1, 1), rows, K), BF16),
                pltpu.VMEM((2, max(Z - 1, 1), rows, K), BF16),
                pltpu.VMEM((nr, rows, K), BF16),
                dma(7), dma(2),
                dma(Z - 1), dma(Z - 1),
                dma((Y - 1) * Z), dma((Y - 1) * Z),
                dma(Y * Z), dma(Y * Z),
                dma(nr - 1), dma(nr - 1),
                dma(nr - 1), dma(nr - 1),
                dma(2), dma(2),
                dma(2 * Y * Z), dma(2 * Y * Z),
                dma(2 * Z), dma(2 * Z),
                dma(nr - 1), dma(nr - 1),
            ],
            compiler_params=pltpu.CompilerParams(
                collective_id=0, has_side_effects=True, vmem_limit_bytes=67043328
            ),
            name="likelihood_backward",
        )(whiten, leaf_root, leaf_region, root_factor, root_adjoint, region_factor, region_adjoint)
        return pl.pallas_call(
            store,
            out_shape=tuple(jax.ShapeDtypeStruct(x.shape, x.dtype) for x in held),
            in_specs=[pl.BlockSpec(memory_space=pltpu.HBM)] * 4,
            out_specs=(pl.BlockSpec(memory_space=pltpu.HBM),) * 4,
            scratch_shapes=[pltpu.VMEM(x.shape, x.dtype) for x in held] + [dma(2 * pl.cdiv(obs, 256) + 2)] * 2,
            compiler_params=pltpu.CompilerParams(vmem_limit_bytes=67043328),
            name="store_outputs",
        )(*held)

    return jax.shard_map(
        on_device,
        mesh=mesh,
        in_specs=(
            P(("region", "leaf"), None, None),
            P(("region", "leaf"), None, None),
            P(("region", "leaf"), None, None),
            P("region", None),
            P("region", None),
            P("region", "leaf", None),
            P("region", "leaf", None),
        ),
        out_specs=(
            P(("region", "leaf"), None, None),
            P(("region", "leaf"), None, None),
            P("leaf", None),
            P("region", "leaf", None),
        ),
        check_vma=False,
    )
```

profile of v0, /device:TPU:0, one launch (start us, length us, event | category | flops | bytes accessed | tf_op | source)
XLA Modules:
  0.0 29.9 jit_solution(17237640964656871959)
XLA Ops:
  0.6 26.8 %likelihood_backward.1 = (bf16[1,1024,512]{2,1,0:T(8,128)(2,1)}, bf16[1,1024,512]{2,1,0:T(8,128)(2,1)}, f32[32,512]{1,0:T(8,128)}, f32[1,32,512]{2,1,0:T(8,128)}) custom-call(bf16[1,1024,1024]{2,1,0:T(8,128)(2,1)} %w_in.1, bf16[1,1024,512]{2,1,0:T(8,128)(2,1)} %lr_in.1, bf16[1,1024,512]{2,1,0:T(8,128)(2,1)} %lg_in.1, bf16[256,512]{1,0:T(8,128)(2,1)} %rf_in.1, ...), custom_call_target="tpu_custom_call" | custom-call | tf_op jit(solution)/shard_map/likelihood_backward/pallas_call | solution.py:309
  27.4 2.5 %store_outputs.1 = (bf16[1,1024,512]{2,1,0:T(8,128)(2,1)}, bf16[1,1024,512]{2,1,0:T(8,128)(2,1)}, f32[32,512]{1,0:T(8,128)}, f32[1,32,512]{2,1,0:T(8,128)}) custom-call(bf16[1,1024,512]{2,1,0:T(8,128)(2,1)} %get-tuple-element.8.refs_0_, bf16[1,1024,512]{2,1,0:T(8,128)(2,1)} %get-tuple-element.9.refs_1_, f32[32,512]{1,0:T(8,128)} %get-tuple-element.10.refs_2_, ...), custom_call_target="tpu_custom_call" | custom-call | tf_op jit(solution)/shard_map/store_outputs/pallas_call | solution.py:351
where the time goes:
time: 30 us; the launch traced here: 29.9 us
  Pallas kernels  29.2 us (97%)
  between operations  0.64 us (2%)
    pallas_call x1, Pallas kernels, on_device(): pl.pallas_call(functools.partial(kernel, nr, nl), out_shape=(jax.ShapeDty...  26.8 us
    pallas_call x1, Pallas kernels, on_device(): pl.pallas_call(store, out_shape=tuple((jax.ShapeDtypeStruct(x.shape, x.dt...  2.47 us

commit v1 on v0

--- a/solution.py
+++ b/solution.py
@@ -38,8 +38,8 @@
     nr, nl,
     w_in, lr_in, lg_in, rf_in, ra_in, gf_in, ga_in,
     gr_out, gg_out, fr_out, fg_out,
-    w, l, a, b, rt, rg, g, grad, cb, rc, ys, ry, zs, rz, rx,
-    ld, st, gz_s, gz_r, gy_s, gy_r, gc_s, gc_r, gx_s, gx_r, gp_s, gp_r,
+    w, l, a, b, rt, rg, g, cb, rc, ys, ry, zs, rz, rx,
+    ld, gz_s, gz_r, gy_s, gy_r, gc_s, gc_r, gx_s, gx_r, gp_s, gp_r,
     cs_s, cs_r, ys_s, ys_r, zs_s, zs_r, xs_s, xs_r,
 ):
     Z, Y = split_leaf(nl)
@@ -217,10 +217,7 @@
     def make_grad(p, out):
         for i in range(nb):
             part = pl.ds(i * T, T)
-            grad[p, part, :] = dot(b[p, part, :], g[p]).astype(BF16)
-        copy = pltpu.make_async_copy(grad.at[p], out.at[0], st.at[p])
-        copy.start()
-        return copy
+            out[0, part, :] = dot(b[p, part, :], g[p]).astype(BF16)
 
     loads[4].wait()
     loads[5].wait()
@@ -257,13 +254,13 @@
     rx[r] = finish_z(0).astype(BF16)
     for k in range(1, nr):
         send(rx.at[r], rx.at[r], xs_s.at[k - 1], xs_r.at[k - 1], {"region": rp(k)})
-    stores = [make_grad(0, gr_out)]
+    make_grad(0, gr_out)
     for ky in range(Y):
         for kz in range(Z):
             i = ky * Z + kz
             arrive(block(kz, ky, oc), gc_s.at[i], gc_r.at[i], other)
     make_g(1, rg)
-    stores.append(make_grad(1, gg_out))
+    make_grad(1, gg_out)
     fg_out[0] = dot(finish_z(1).astype(BF16), g[1])
     for k in range(1, nr):
         arrive(rx.at[rm(k)], xs_s.at[k - 1], xs_r.at[k - 1], other)
@@ -271,28 +268,14 @@
     for k in range(1, nr):
         total += rx[k].astype(F32)
     fr_out[...] = dot(total.astype(BF16), g[0])
-    for copy in stores:
-        copy.wait()
     for copy in sends:
         copy.wait_send()
 
 
 def store(*refs):
-    source, target, held = refs[:4], refs[4:8], refs[8:12]
-    load_sem, store_sem = refs[12:]
-    pieces = []
-    for n in range(4):
-        extent = source[n].shape[-2]
-        size = min(extent, 256)
-        for row in range(0, extent, size):
-            where = (pl.ds(row, size),) if len(source[n].shape) == 2 else (0, pl.ds(row, size))
-            pieces.append((source[n].at[where], held[n].at[where], target[n].at[where]))
-    loads = [pltpu.make_async_copy(p[0], p[1], load_sem.at[i]) for i, p in enumerate(pieces)]
-    stores = [pltpu.make_async_copy(p[1], p[2], store_sem.at[i]) for i, p in enumerate(pieces)]
-    for load in loads:
-        load.start()
-    for load, save in zip(loads, stores):
-        load.wait()
+    held, target, store_sem = refs[:4], refs[4:8], refs[8]
+    stores = [pltpu.make_async_copy(held[n], target[n], store_sem.at[n]) for n in range(4)]
+    for save in stores:
         save.start()
     for save in stores:
         save.wait()
@@ -306,6 +289,8 @@
         obs, K = leaf_root.shape[1], leaf_root.shape[2]
         rows = K // nl
         dma = lambda n: pltpu.SemaphoreType.DMA((max(n, 1),))
+        args = [pltpu.with_memory_space_constraint(x, pltpu.HBM) for x in (
+            whiten, leaf_root, leaf_region, root_factor, root_adjoint, region_factor, region_adjoint)]
         held = pl.pallas_call(
             functools.partial(kernel, nr, nl),
             out_shape=(
@@ -315,7 +300,7 @@
                 jax.ShapeDtypeStruct((1, rows, K), F32),
             ),
             in_specs=[pl.BlockSpec(memory_space=pltpu.HBM)] * 7,
-            out_specs=(pl.BlockSpec(memory_space=pltpu.HBM),) * 2 + (pl.BlockSpec(memory_space=pltpu.VMEM),) * 2,
+            out_specs=(pl.BlockSpec(memory_space=pltpu.VMEM),) * 4,
             scratch_shapes=[
                 pltpu.VMEM((obs, obs), BF16),
                 pltpu.VMEM((2, obs, K), BF16),
@@ -324,7 +309,6 @@
                 pltpu.VMEM((2, K, K), BF16),
                 pltpu.VMEM((2, K, K), BF16),
                 pltpu.VMEM((2, K, K), BF16),
-                pltpu.VMEM((2, obs, K), BF16),
                 pltpu.VMEM((2, Z, Y, 2, rows, K), BF16),
                 pltpu.VMEM((2, Z, Y, rows, K), BF16),
                 pltpu.VMEM((2, max(Y - 1, 1), Z, rows, K), BF16),
@@ -332,7 +316,7 @@
                 pltpu.VMEM((2, max(Z - 1, 1), rows, K), BF16),
                 pltpu.VMEM((2, max(Z - 1, 1), rows, K), BF16),
                 pltpu.VMEM((nr, rows, K), BF16),
-                dma(7), dma(2),
+                dma(7),
                 dma(Z - 1), dma(Z - 1),
                 dma((Y - 1) * Z), dma((Y - 1) * Z),
                 dma(Y * Z), dma(Y * Z),
@@ -344,17 +328,17 @@
                 dma(nr - 1), dma(nr - 1),
             ],
             compiler_params=pltpu.CompilerParams(
-                collective_id=0, has_side_effects=True, vmem_limit_bytes=67043328
+                collective_id=0, has_side_effects=True, vmem_limit_bytes=40 << 20
             ),
             name="likelihood_backward",
-        )(whiten, leaf_root, leaf_region, root_factor, root_adjoint, region_factor, region_adjoint)
+        )(*args)
         return pl.pallas_call(
             store,
             out_shape=tuple(jax.ShapeDtypeStruct(x.shape, x.dtype) for x in held),
-            in_specs=[pl.BlockSpec(memory_space=pltpu.HBM)] * 4,
+            in_specs=[pl.BlockSpec(memory_space=pltpu.VMEM)] * 4,
             out_specs=(pl.BlockSpec(memory_space=pltpu.HBM),) * 4,
-            scratch_shapes=[pltpu.VMEM(x.shape, x.dtype) for x in held] + [dma(2 * pl.cdiv(obs, 256) + 2)] * 2,
-            compiler_params=pltpu.CompilerParams(vmem_limit_bytes=67043328),
+            scratch_shapes=[dma(4)],
+            compiler_params=pltpu.CompilerParams(vmem_limit_bytes=1 << 20),
             name="store_outputs",
         )(*held)
 

time: 30 us -> 28.2 us (0.940)
  Pallas kernels: 29.2 us -> 27.4 us
    pallas_call x1, Pallas kernels: 2.47 us -> 1.38 us  [on_device(): pl.pallas_call(store, out_shape=tuple((jax.ShapeDtypeStruct(x.shape, x.dt...]
    pallas_call x1, Pallas kernels: 26.8 us -> 26.1 us  [on_device(): pl.pallas_call(functools.partial(kernel, nr, nl), out_shape=(jax.ShapeDty...]
where the time goes in v1:
time: 28.2 us; the launch traced here: 28.1 us
  Pallas kernels  27.4 us (97%)
  between operations  0.64 us (2%)
    pallas_call x1, Pallas kernels, on_device(): pl.pallas_call(functools.partial(kernel, nr, nl), out_shape=(jax.ShapeDty...  26.1 us
    pallas_call x1, Pallas kernels, on_device(): pl.pallas_call(store, out_shape=tuple((jax.ShapeDtypeStruct(x.shape, x.dt...  1.38 us

profile of v1, /device:TPU:0, one launch (start us, length us, event | category | flops | bytes accessed | tf_op | source)
XLA Modules:
  0.0 28.1 jit_solution(17215146240507874149)
XLA Ops:
  0.6 26.1 %likelihood_backward.1 = (bf16[1,1024,512]{2,1,0:T(8,128)(2,1)S(1)}, bf16[1,1024,512]{2,1,0:T(8,128)(2,1)S(1)}, f32[32,512]{1,0:T(8,128)S(1)}, f32[1,32,512]{2,1,0:T(8,128)S(1)}) custom-call(bf16[1,1024,1024]{2,1,0:T(8,128)(2,1)} %w_in.1, bf16[1,1024,512]{2,1,0:T(8,128)(2,1)} %lr_in.1, bf16[1,1024,512]{2,1,0:T(8,128)(2,1)} %lg_in.1, bf16[256,512]{1,0:T(8,128)(2,1)} %rf_in.1, ...), custom_call_target="tpu_custom_call" | custom-call | tf_op jit(solution)/shard_map/likelihood_backward/pallas_call | solution.py:294
  26.7 1.4 %store_outputs.1 = (bf16[1,1024,512]{2,1,0:T(8,128)(2,1)}, bf16[1,1024,512]{2,1,0:T(8,128)(2,1)}, f32[32,512]{1,0:T(8,128)}, f32[1,32,512]{2,1,0:T(8,128)}) custom-call(bf16[1,1024,512]{2,1,0:T(8,128)(2,1)S(1)} %get-tuple-element.8.refs_0_, bf16[1,1024,512]{2,1,0:T(8,128)(2,1)S(1)} %get-tuple-element.9.refs_1_, f32[32,512]{1,0:T(8,128)S(1)} %get-tuple-element.10.refs_2_, ...), custom_call_target="tpu_custom_call" | custom-call | tf_op jit(solution)/shard_map/store_outputs/pallas_call | solution.py:335

commit v2 on v1

--- a/solution.py
+++ b/solution.py
@@ -39,8 +39,8 @@
     w_in, lr_in, lg_in, rf_in, ra_in, gf_in, ga_in,
     gr_out, gg_out, fr_out, fg_out,
     w, l, a, b, rt, rg, g, cb, rc, ys, ry, zs, rz, rx,
-    ld, gz_s, gz_r, gy_s, gy_r, gc_s, gc_r, gx_s, gx_r, gp_s, gp_r,
-    cs_s, cs_r, ys_s, ys_r, zs_s, zs_r, xs_s, xs_r,
+    ld, lb, gz_s, gz_r, gy_s, gy_r, gc_s, gc_r, gx_s, gx_r, gp_s, gp_r,
+    cs_s, cs_r, ys_s, ys_r, zs_s, zs_r, xs_s, xs_r, zn, yn, cn, xn,
 ):
     Z, Y = split_leaf(nl)
     obs, K = l.shape[1], l.shape[2]
@@ -72,33 +72,50 @@
     def rm(k):
         return lax.rem(r + nr - k, nr)
 
+    def back(k, count):
+        return count - k if count & (count - 1) else k
+
     def span(index, size):
         return pl.ds(pl.multiple_of(index * size, size), size)
 
     mine = span(leaf, rows)
     own = span(r, half)
-    loads = [
+    first = [
         pltpu.make_async_copy(gf_in.at[0], rg.at[0, mine], ld.at[0]),
         pltpu.make_async_copy(ga_in.at[0], rg.at[1, mine], ld.at[1]),
+    ]
+    halves = [
         pltpu.make_async_copy(rf_in, rt.at[0, own], ld.at[2]),
         pltpu.make_async_copy(ra_in, rt.at[1, own], ld.at[3]),
-        pltpu.make_async_copy(lr_in.at[0], l.at[0], ld.at[4]),
-        pltpu.make_async_copy(w_in.at[0], w, ld.at[5]),
-        pltpu.make_async_copy(lg_in.at[0], l.at[1], ld.at[6]),
     ]
-    for load in loads:
+    bands = []
+    for i in range(nb):
+        band, left = pl.ds(i * T, T), pl.ds(0, (i + 1) * T)
+        bands.append([
+            pltpu.make_async_copy(w_in.at[0, band, left], w.at[band, left], lb.at[0, i]),
+            pltpu.make_async_copy(lr_in.at[0, band], l.at[0, band], lb.at[1, i]),
+        ])
+    second = pltpu.make_async_copy(lg_in.at[0], l.at[1], ld.at[4])
+    for load in first + sum(bands, []) + halves + [second]:
         load.start()
 
+    other = {"leaf": at(z, y, oc)}
+    z_peers = [({"leaf": at(zp(k), y, c)}, zp(k) > z, zn.at[k - 1], zn.at[back(k, Z) - 1]) for k in range(1, Z)]
+    y_peers = [({"leaf": at(z, yp(k), c)}, yp(k) > y, yn.at[k - 1], yn.at[back(k, Y) - 1]) for k in range(1, Y)]
+    x_peers = [({"region": rp(k)}, rp(k) > r, xn.at[k - 1], xn.at[nr - k - 1]) for k in range(1, nr)]
+    c_peers = [(other, oc > c, cn.at[0], cn.at[0])]
+    peers = z_peers + y_peers + x_peers + c_peers
+
     barrier = pltpu.get_barrier_semaphore()
-    peers = [{"leaf": at(zp(k), y, c)} for k in range(1, Z)]
-    peers += [{"leaf": at(z, yp(k), c)} for k in range(1, Y)]
-    peers += [{"leaf": at(z, y, oc)}]
-    peers += [{"region": rp(k)} for k in range(1, nr)]
-    for peer in peers:
-        pl.semaphore_signal(barrier, inc=1, device_id=peer, device_id_type=MESH)
-    for load in loads[:4]:
-        load.wait()
-    pl.semaphore_wait(barrier, len(peers))
+    for peer, later, _, _ in peers:
+        @pl.when(later)
+        def _():
+            pl.semaphore_signal(barrier, inc=1, device_id=peer, device_id_type=MESH)
+    pl.when(leaf + r > 0)(lambda: pl.semaphore_wait(barrier, z + y + r + c))
+    for peer, later, _, theirs in peers:
+        @pl.when(jnp.logical_not(later))
+        def _():
+            pl.semaphore_signal(theirs, inc=1, device_id=peer, device_id_type=MESH)
 
     sends = []
 
@@ -108,64 +125,76 @@
             device_id=peer, device_id_type=MESH,
         )
 
-    def send(src, dst, ssem, rsem, peer):
+    def plan(src, dst, ssem, rsem, peer):
         copy = remote(src, dst, ssem, rsem, peer)
-        copy.start()
         sends.append(copy)
-
-    def arrive(ref, ssem, rsem, peer):
-        remote(ref, ref, ssem, rsem, peer).wait_recv()
-
-    other = {"leaf": at(z, y, oc)}
+        return copy
+
+    def send(*args):
+        plan(*args).start()
+
+    def arrive(ref, ssem, rsem):
+        remote(ref, ref, ssem, rsem, other).wait_recv()
 
     def block(kz, ky, cc):
         return rg.at[:, span(at(zm(kz), ym(ky), cc), rows)]
 
     def gather_y(kz):
-        for ky in range(1, Y):
-            i = (ky - 1) * Z + kz
-            send(block(kz, 0, c), block(kz, 0, c), gy_s.at[i], gy_r.at[i], {"leaf": at(z, yp(ky), c)})
+        return [
+            (plan(block(kz, 0, c), block(kz, 0, c), gy_s.at[(ky - 1) * Z + kz], gy_r.at[(ky - 1) * Z + kz],
+                  {"leaf": at(z, yp(ky), c)}))
+            for ky in range(1, Y)
+        ]
 
     def gather_core(kz, ky):
         i = ky * Z + kz
-        send(block(kz, ky, c), block(kz, ky, c), gc_s.at[i], gc_r.at[i], other)
+        return plan(block(kz, ky, c), block(kz, ky, c), gc_s.at[i], gc_r.at[i], other)
 
     def z_forward(kz):
-        arrive(block(kz, 0, c), gz_s.at[kz - 1], gz_r.at[kz - 1], other)
-        gather_y(kz)
-        gather_core(kz, 0)
+        arrive(block(kz, 0, c), gz_s.at[kz - 1], gz_r.at[kz - 1])
+        for copy in gather_y(kz):
+            copy.start()
+        gather_core(kz, 0).start()
 
     def y_forward(kz, ky):
         i = (ky - 1) * Z + kz
-        arrive(block(kz, ky, c), gy_s.at[i], gy_r.at[i], other)
-        gather_core(kz, ky)
-
-    for k in range(1, Z):
-        send(block(0, 0, c), block(0, 0, c), gz_s.at[k - 1], gz_r.at[k - 1], {"leaf": at(zp(k), y, c)})
-    gather_y(0)
-    for k in range(1, nr):
-        send(rt.at[c, own], rt.at[c, own], gx_s.at[k - 1], gx_r.at[k - 1], {"region": rp(k)})
-    gather_core(0, 0)
+        arrive(block(kz, ky, c), gy_s.at[i], gy_r.at[i])
+        gather_core(kz, ky).start()
+
+    to_z = [plan(block(0, 0, c), block(0, 0, c), gz_s.at[k - 1], gz_r.at[k - 1], z_peers[k - 1][0]) for k in range(1, Z)]
+    to_y = gather_y(0)
+    to_c = [gather_core(0, 0)]
+    to_x = [plan(rt.at[c, own], rt.at[c, own], gx_s.at[k - 1], gx_r.at[k - 1], x_peers[k - 1][0]) for k in range(1, nr)]
+
+    def open_early(group, copies):
+        for (_, later, _, _), copy in zip(group, copies):
+            pl.when(jnp.logical_not(later))(copy.start)
+
+    def open_late(group, copies):
+        for (_, later, sem, _), copy in zip(group, copies):
+            @pl.when(later)
+            def _():
+                pl.semaphore_wait(sem, 1)
+                copy.start()
 
     scale = 1.0 / obs
 
-    def local_a(p):
-        for n in range(K // T):
-            cols = pl.ds(n * T, T)
-            for i in range(nb):
-                a[p, pl.ds(i * T, T), cols] = dot(
-                    w[pl.ds(i * T, T), pl.ds(0, (i + 1) * T)], l[p, pl.ds(0, (i + 1) * T), cols]
-                ).astype(BF16)
+    def a_band(p, i):
+        a[p, pl.ds(i * T, T), :] = dot(
+            w[pl.ds(i * T, T), pl.ds(0, (i + 1) * T)], l[p, pl.ds(0, (i + 1) * T), :]
+        ).astype(BF16)
+
+    step = max(T, 2 * Y * rows)
+    per = step // (2 * Y * rows)
+    parts = K // step
 
     def local_c(p):
-        per = T // (2 * Y * rows) if T >= 2 * Y * rows else 0
-        step = T if per else 2 * Y * rows
-        per = step // (2 * Y * rows)
-        for i in range(K // step):
+        for i in range(parts):
             left = a[p, :, pl.ds(i * step, step)].T
             part = (dot(left, a[p]) * scale).astype(BF16)
-            cb[p, pl.ds(i * per, per)] = part.reshape(per, Y, 2, rows, K)
-        send(cb.at[p, :, :, oc], rc.at[p], cs_s.at[p], cs_r.at[p], other)
+            here = pl.ds(i * per, per)
+            cb[p, here] = part.reshape(per, Y, 2, rows, K)
+            send(cb.at[p, here, :, oc], rc.at[p, here], cs_s.at[p * parts + i], cs_r.at[p * parts + i], other)
 
     def local_b(i):
         left = w[pl.ds(i * T, obs - i * T), pl.ds(i * T, T)].T
@@ -173,23 +202,31 @@
             b[p, pl.ds(i * T, T), :] = dot(left, a[p, pl.ds(i * T, obs - i * T), :]).astype(BF16)
 
     far = range(Z - 1, -1, -1)
+    y_sends = {}
+    for p in range(2):
+        for kz in far:
+            for k in range(1, Y):
+                i = (p * Y + k) * Z + kz
+                y_sends[p, kz, k] = plan(
+                    ys.at[p, k - 1, kz], ry.at[p, k - 1, kz], ys_s.at[i], ys_r.at[i], {"leaf": at(z, yp(k), c)}
+                )
 
     def reduce_y(p):
-        arrive(rc.at[p], cs_s.at[p], cs_r.at[p], other)
+        for i in range(parts):
+            arrive(rc.at[p, pl.ds(i * per, per)], cs_s.at[p * parts + i], cs_r.at[p * parts + i])
         for kz in far:
             zz = zp(kz)
             for k in range(1, Y):
                 yy = yp(k)
                 ys[p, k - 1, kz] = (cb[p, zz, yy, c].astype(F32) + rc[p, zz, yy].astype(F32)).astype(BF16)
-                i = (p * Y + k) * Z + kz
-                send(ys.at[p, k - 1, kz], ry.at[p, k - 1, kz], ys_s.at[i], ys_r.at[i], {"leaf": at(z, yy, c)})
+                y_sends[p, kz, k].start()
 
     def chip_sum(p, kz):
         zz = zp(kz)
         total = cb[p, zz, y, c].astype(F32) + rc[p, zz, y].astype(F32)
         for k in range(1, Y):
             i = (p * Y + k) * Z + kz
-            arrive(ry.at[p, k - 1, kz], ys_s.at[i], ys_r.at[i], other)
+            arrive(ry.at[p, k - 1, kz], ys_s.at[i], ys_r.at[i])
             total += ry[p, k - 1, kz].astype(F32)
         return total
 
@@ -203,7 +240,7 @@
         total = chip_sum(p, 0)
         for k in range(1, Z):
             i = p * Z + k
-            arrive(rz.at[p, k - 1], zs_s.at[i], zs_r.at[i], other)
+            arrive(rz.at[p, k - 1], zs_s.at[i], zs_r.at[i])
             total += rz[p, k - 1].astype(F32)
         return total
 
@@ -219,22 +256,38 @@
             part = pl.ds(i * T, T)
             out[0, part, :] = dot(b[p, part, :], g[p]).astype(BF16)
 
-    loads[4].wait()
-    loads[5].wait()
-    local_a(0)
+    for load in first:
+        load.wait()
+    open_early(z_peers, to_z)
+    open_early(y_peers, to_y)
+    open_early(c_peers, to_c)
+    for i in range(nb):
+        for load in bands[i]:
+            load.wait()
+        a_band(0, i)
+    open_late(c_peers, to_c)
     local_c(0)
+    for load in halves:
+        load.wait()
+    open_early(x_peers, to_x)
+    open_late(y_peers, to_y)
+    open_late(z_peers, to_z)
+    open_late(x_peers, to_x)
+    pl.when(c == 1)(lambda: reduce_y(0))
+    second.wait()
+    for i in range(nb):
+        a_band(1, i)
+    local_c(1)
+    pl.when(c == 1)(lambda: reduce_y(1))
     if Z > 1:
         z_forward(1)
-    loads[6].wait()
-    local_a(1)
-    local_c(1)
+    pl.when(c == 0)(lambda: reduce_y(0))
     if Z > 2:
         z_forward(2)
     local_b(0)
-    reduce_y(0)
     for k in range(3, Z):
         z_forward(k)
-    reduce_y(1)
+    pl.when(c == 0)(lambda: reduce_y(1))
     for i in range(1, nb):
         local_b(i)
     for ky in range(1, Y):
@@ -242,14 +295,14 @@
     reduce_z(0)
     for k in range(1, nr):
         theirs = rt.at[c, span(rm(k), half)]
-        arrive(theirs, gx_s.at[k - 1], gx_r.at[k - 1], other)
+        arrive(theirs, gx_s.at[k - 1], gx_r.at[k - 1])
         send(theirs, theirs, gp_s.at[k - 1], gp_r.at[k - 1], other)
     for ky in range(1, Y):
         for k in range(1, Z):
             y_forward(k, ky)
     reduce_z(1)
     for k in range(1, nr):
-        arrive(rt.at[oc, span(rm(k), half)], gp_s.at[k - 1], gp_r.at[k - 1], other)
+        arrive(rt.at[oc, span(rm(k), half)], gp_s.at[k - 1], gp_r.at[k - 1])
     make_g(0, rt)
     rx[r] = finish_z(0).astype(BF16)
     for k in range(1, nr):
@@ -258,12 +311,12 @@
     for ky in range(Y):
         for kz in range(Z):
             i = ky * Z + kz
-            arrive(block(kz, ky, oc), gc_s.at[i], gc_r.at[i], other)
+            arrive(block(kz, ky, oc), gc_s.at[i], gc_r.at[i])
     make_g(1, rg)
     make_grad(1, gg_out)
     fg_out[0] = dot(finish_z(1).astype(BF16), g[1])
     for k in range(1, nr):
-        arrive(rx.at[rm(k)], xs_s.at[k - 1], xs_r.at[k - 1], other)
+        arrive(rx.at[rm(k)], xs_s.at[k - 1], xs_r.at[k - 1])
     total = rx[0].astype(F32)
     for k in range(1, nr):
         total += rx[k].astype(F32)
@@ -288,7 +341,9 @@
     def on_device(whiten, leaf_root, leaf_region, root_factor, root_adjoint, region_factor, region_adjoint):
         obs, K = leaf_root.shape[1], leaf_root.shape[2]
         rows = K // nl
+        parts = K // max(min(256, K), 2 * Y * rows)
         dma = lambda n: pltpu.SemaphoreType.DMA((max(n, 1),))
+        flag = lambda n: pltpu.SemaphoreType.REGULAR((max(n, 1),))
         args = [pltpu.with_memory_space_constraint(x, pltpu.HBM) for x in (
             whiten, leaf_root, leaf_region, root_factor, root_adjoint, region_factor, region_adjoint)]
         held = pl.pallas_call(
@@ -316,16 +371,17 @@
                 pltpu.VMEM((2, max(Z - 1, 1), rows, K), BF16),
                 pltpu.VMEM((2, max(Z - 1, 1), rows, K), BF16),
                 pltpu.VMEM((nr, rows, K), BF16),
-                dma(7),
+                dma(5), pltpu.SemaphoreType.DMA((2, obs // min(256, K))),
                 dma(Z - 1), dma(Z - 1),
                 dma((Y - 1) * Z), dma((Y - 1) * Z),
                 dma(Y * Z), dma(Y * Z),
                 dma(nr - 1), dma(nr - 1),
                 dma(nr - 1), dma(nr - 1),
-                dma(2), dma(2),
+                dma(2 * parts), dma(2 * parts),
                 dma(2 * Y * Z), dma(2 * Y * Z),
                 dma(2 * Z), dma(2 * Z),
                 dma(nr - 1), dma(nr - 1),
+                flag(Z - 1), flag(Y - 1), flag(1), flag(nr - 1),
             ],
             compiler_params=pltpu.CompilerParams(
                 collective_id=0, has_side_effects=True, vmem_limit_bytes=40 << 20

time: 28.2 us -> 26.8 us (0.950)
  Pallas kernels: 27.4 us -> 26 us
    pallas_call x1, Pallas kernels: 26.1 us -> 24.7 us  [on_device(): pl.pallas_call(functools.partial(kernel, nr, nl), out_shape=(jax.ShapeDty...]
where the time goes in v2:
time: 26.8 us; the launch traced here: 26.7 us
  Pallas kernels  26 us (97%)
  between operations  0.64 us (2%)
    pallas_call x1, Pallas kernels, on_device(): pl.pallas_call(functools.partial(kernel, nr, nl), out_shape=(jax.ShapeDty...  24.7 us
    pallas_call x1, Pallas kernels, on_device(): pl.pallas_call(store, out_shape=tuple((jax.ShapeDtypeStruct(x.shape, x.dt...  1.38 us

profile of v2, /device:TPU:0, one launch (start us, length us, event | category | flops | bytes accessed | tf_op | source)
XLA Modules:
  0.0 26.7 jit_solution(7439225075641792053)
XLA Ops:
  0.6 24.7 %likelihood_backward.1 = (bf16[1,1024,512]{2,1,0:T(8,128)(2,1)S(1)}, bf16[1,1024,512]{2,1,0:T(8,128)(2,1)S(1)}, f32[32,512]{1,0:T(8,128)S(1)}, f32[1,32,512]{2,1,0:T(8,128)S(1)}) custom-call(bf16[1,1024,1024]{2,1,0:T(8,128)(2,1)} %w_in.1, bf16[1,1024,512]{2,1,0:T(8,128)(2,1)} %lr_in.1, bf16[1,1024,512]{2,1,0:T(8,128)(2,1)} %lg_in.1, bf16[256,512]{1,0:T(8,128)(2,1)} %rf_in.1, ...), custom_call_target="tpu_custom_call" | custom-call | tf_op jit(solution)/shard_map/likelihood_backward/pallas_call | solution.py:349
  25.3 1.4 %store_outputs.1 = (bf16[1,1024,512]{2,1,0:T(8,128)(2,1)}, bf16[1,1024,512]{2,1,0:T(8,128)(2,1)}, f32[32,512]{1,0:T(8,128)}, f32[1,32,512]{2,1,0:T(8,128)}) custom-call(bf16[1,1024,512]{2,1,0:T(8,128)(2,1)S(1)} %get-tuple-element.8.refs_0_, bf16[1,1024,512]{2,1,0:T(8,128)(2,1)S(1)} %get-tuple-element.9.refs_1_, f32[32,512]{1,0:T(8,128)S(1)} %get-tuple-element.10.refs_2_, ...), custom_call_target="tpu_custom_call" | custom-call | tf_op jit(solution)/shard_map/store_outputs/pallas_call | solution.py:391

commit v3 on v2

--- a/solution.py
+++ b/solution.py
@@ -39,8 +39,7 @@
     w_in, lr_in, lg_in, rf_in, ra_in, gf_in, ga_in,
     gr_out, gg_out, fr_out, fg_out,
     w, l, a, b, rt, rg, g, cb, rc, ys, ry, zs, rz, rx,
-    ld, lb, gz_s, gz_r, gy_s, gy_r, gc_s, gc_r, gx_s, gx_r, gp_s, gp_r,
-    cs_s, cs_r, ys_s, ys_r, zs_s, zs_r, xs_s, xs_r, zn, yn, cn, xn,
+    ld, lb, out_sem, gz, gy, gc, gx, gp, cs, yr, zr, xr, zn, yn, cn, xn,
 ):
     Z, Y = split_leaf(nl)
     obs, K = l.shape[1], l.shape[2]
@@ -80,24 +79,22 @@
 
     mine = span(leaf, rows)
     own = span(r, half)
-    first = [
-        pltpu.make_async_copy(gf_in.at[0], rg.at[0, mine], ld.at[0]),
-        pltpu.make_async_copy(ga_in.at[0], rg.at[1, mine], ld.at[1]),
-    ]
-    halves = [
-        pltpu.make_async_copy(rf_in, rt.at[0, own], ld.at[2]),
-        pltpu.make_async_copy(ra_in, rt.at[1, own], ld.at[3]),
-    ]
+    def copies(sem, *pairs):
+        return [pltpu.make_async_copy(src, dst, sem) for src, dst in pairs]
+
+    first = copies(ld.at[0], (gf_in.at[0], rg.at[0, mine]), (ga_in.at[0], rg.at[1, mine]))
+    halves = copies(ld.at[1], (rf_in, rt.at[0, own]), (ra_in, rt.at[1, own]))
     bands = []
     for i in range(nb):
         band, left = pl.ds(i * T, T), pl.ds(0, (i + 1) * T)
-        bands.append([
-            pltpu.make_async_copy(w_in.at[0, band, left], w.at[band, left], lb.at[0, i]),
-            pltpu.make_async_copy(lr_in.at[0, band], l.at[0, band], lb.at[1, i]),
-        ])
-    second = pltpu.make_async_copy(lg_in.at[0], l.at[1], ld.at[4])
-    for load in first + sum(bands, []) + halves + [second]:
+        bands.append(copies(lb.at[i], (w_in.at[0, band, left], w.at[band, left]), (lr_in.at[0, band], l.at[0, band])))
+    second = copies(ld.at[2], (lg_in.at[0], l.at[1]))
+    for load in first + sum(bands, []) + halves + second:
         load.start()
+
+    def taken(sem, count):
+        whole = l.at[0, pl.ds(0, count)] if count <= obs else l.at[:, pl.ds(0, count // 2)]
+        pltpu.make_async_copy(whole, whole, sem).wait()
 
     other = {"leaf": at(z, y, oc)}
     z_peers = [({"leaf": at(zp(k), y, c)}, zp(k) > z, zn.at[k - 1], zn.at[back(k, Z) - 1]) for k in range(1, Z)]
@@ -117,54 +114,43 @@
         def _():
             pl.semaphore_signal(theirs, inc=1, device_id=peer, device_id_type=MESH)
 
-    sends = []
-
-    def remote(src, dst, ssem, rsem, peer):
+    sent = [0, 0]
+
+    def plan(kind, src, dst, rsem, peer):
+        sent[kind] += math.prod(src.shape) // K
         return pltpu.make_async_remote_copy(
-            src_ref=src, dst_ref=dst, send_sem=ssem, recv_sem=rsem,
+            src_ref=src, dst_ref=dst, send_sem=out_sem.at[kind], recv_sem=rsem,
             device_id=peer, device_id_type=MESH,
         )
 
-    def plan(src, dst, ssem, rsem, peer):
-        copy = remote(src, dst, ssem, rsem, peer)
-        sends.append(copy)
-        return copy
-
     def send(*args):
         plan(*args).start()
 
-    def arrive(ref, ssem, rsem):
-        remote(ref, ref, ssem, rsem, other).wait_recv()
-
     def block(kz, ky, cc):
         return rg.at[:, span(at(zm(kz), ym(ky), cc), rows)]
 
-    def gather_y(kz):
+    def to_ys(kz):
         return [
-            (plan(block(kz, 0, c), block(kz, 0, c), gy_s.at[(ky - 1) * Z + kz], gy_r.at[(ky - 1) * Z + kz],
-                  {"leaf": at(z, yp(ky), c)}))
-            for ky in range(1, Y)
+            plan(0, block(kz, 0, c), block(kz, 0, c), gy.at[(k - 1) * Z + kz], {"leaf": at(z, yp(k), c)})
+            for k in range(1, Y)
         ]
 
-    def gather_core(kz, ky):
-        i = ky * Z + kz
-        return plan(block(kz, ky, c), block(kz, ky, c), gc_s.at[i], gc_r.at[i], other)
-
-    def z_forward(kz):
-        arrive(block(kz, 0, c), gz_s.at[kz - 1], gz_r.at[kz - 1])
-        for copy in gather_y(kz):
+    def to_core(kz, ky):
+        return plan(0, block(kz, ky, c), block(kz, ky, c), gc.at[0], other)
+
+    def from_z(kz):
+        taken(gz.at[kz - 1], 2 * rows)
+        for copy in to_ys(kz) + [to_core(kz, 0)]:
             copy.start()
-        gather_core(kz, 0).start()
-
-    def y_forward(kz, ky):
-        i = (ky - 1) * Z + kz
-        arrive(block(kz, ky, c), gy_s.at[i], gy_r.at[i])
-        gather_core(kz, ky).start()
-
-    to_z = [plan(block(0, 0, c), block(0, 0, c), gz_s.at[k - 1], gz_r.at[k - 1], z_peers[k - 1][0]) for k in range(1, Z)]
-    to_y = gather_y(0)
-    to_c = [gather_core(0, 0)]
-    to_x = [plan(rt.at[c, own], rt.at[c, own], gx_s.at[k - 1], gx_r.at[k - 1], x_peers[k - 1][0]) for k in range(1, nr)]
+
+    def from_y(kz, ky):
+        taken(gy.at[(ky - 1) * Z + kz], 2 * rows)
+        to_core(kz, ky).start()
+
+    to_z = [plan(0, block(0, 0, c), block(0, 0, c), gz.at[k - 1], z_peers[k - 1][0]) for k in range(1, Z)]
+    to_y = to_ys(0)
+    to_c = [to_core(0, 0)]
+    to_x = [plan(0, rt.at[c, own], rt.at[c, own], gx.at[k - 1], x_peers[k - 1][0]) for k in range(1, nr)]
 
     def open_early(group, copies):
         for (_, later, _, _), copy in zip(group, copies):
@@ -194,7 +180,7 @@
             part = (dot(left, a[p]) * scale).astype(BF16)
             here = pl.ds(i * per, per)
             cb[p, here] = part.reshape(per, Y, 2, rows, K)
-            send(cb.at[p, here, :, oc], rc.at[p, here], cs_s.at[p * parts + i], cs_r.at[p * parts + i], other)
+            send(1, cb.at[p, here, :, oc], rc.at[p, here], cs.at[p], other)
 
     def local_b(i):
         left = w[pl.ds(i * T, obs - i * T), pl.ds(i * T, T)].T
@@ -202,127 +188,103 @@
             b[p, pl.ds(i * T, T), :] = dot(left, a[p, pl.ds(i * T, obs - i * T), :]).astype(BF16)
 
     far = range(Z - 1, -1, -1)
-    y_sends = {}
-    for p in range(2):
-        for kz in far:
-            for k in range(1, Y):
-                i = (p * Y + k) * Z + kz
-                y_sends[p, kz, k] = plan(
-                    ys.at[p, k - 1, kz], ry.at[p, k - 1, kz], ys_s.at[i], ys_r.at[i], {"leaf": at(z, yp(k), c)}
-                )
 
     def reduce_y(p):
-        for i in range(parts):
-            arrive(rc.at[p, pl.ds(i * per, per)], cs_s.at[p * parts + i], cs_r.at[p * parts + i])
+        taken(cs.at[p], K // 2)
         for kz in far:
             zz = zp(kz)
             for k in range(1, Y):
                 yy = yp(k)
                 ys[p, k - 1, kz] = (cb[p, zz, yy, c].astype(F32) + rc[p, zz, yy].astype(F32)).astype(BF16)
-                y_sends[p, kz, k].start()
+                send(1, ys.at[p, k - 1, kz], ry.at[p, k - 1, kz], yr.at[p * Z + kz], {"leaf": at(z, yy, c)})
 
     def chip_sum(p, kz):
         zz = zp(kz)
         total = cb[p, zz, y, c].astype(F32) + rc[p, zz, y].astype(F32)
+        if Y > 1:
+            taken(yr.at[p * Z + kz], (Y - 1) * rows)
         for k in range(1, Y):
-            i = (p * Y + k) * Z + kz
-            arrive(ry.at[p, k - 1, kz], ys_s.at[i], ys_r.at[i])
             total += ry[p, k - 1, kz].astype(F32)
         return total
 
     def reduce_z(p):
         for k in far[:-1]:
             zs[p, k - 1] = chip_sum(p, k).astype(BF16)
-            i = p * Z + k
-            send(zs.at[p, k - 1], rz.at[p, k - 1], zs_s.at[i], zs_r.at[i], {"leaf": at(zp(k), y, c)})
+            send(1, zs.at[p, k - 1], rz.at[p, k - 1], zr.at[p], {"leaf": at(zp(k), y, c)})
 
     def finish_z(p):
         total = chip_sum(p, 0)
+        if Z > 1:
+            taken(zr.at[p], (Z - 1) * rows)
         for k in range(1, Z):
-            i = p * Z + k
-            arrive(rz.at[p, k - 1], zs_s.at[i], zs_r.at[i])
             total += rz[p, k - 1].astype(F32)
         return total
 
     def make_g(p, held):
-        factor, adjoint = held[0], held[1]
-        both = dot(factor, adjoint) + lax.dot_general(
-            factor, adjoint, (((1,), (1,)), ((), ())), preferred_element_type=F32
-        )
-        g[p] = both.astype(BF16)
+        adjoint = held[1].astype(F32)
+        g[p] = dot(held[0], (adjoint + adjoint.T).astype(BF16)).astype(BF16)
 
     def make_grad(p, out):
         for i in range(nb):
             part = pl.ds(i * T, T)
             out[0, part, :] = dot(b[p, part, :], g[p]).astype(BF16)
 
-    for load in first:
-        load.wait()
+    taken(ld.at[0], 2 * rows)
+    open_early(y_peers, to_y)
     open_early(z_peers, to_z)
-    open_early(y_peers, to_y)
     open_early(c_peers, to_c)
     for i in range(nb):
-        for load in bands[i]:
-            load.wait()
+        taken(lb.at[i], (i + 1) * T * T // K + T)
         a_band(0, i)
     open_late(c_peers, to_c)
-    local_c(0)
-    for load in halves:
-        load.wait()
-    open_early(x_peers, to_x)
     open_late(y_peers, to_y)
     open_late(z_peers, to_z)
+    local_c(0)
+    taken(ld.at[1], 2 * half)
+    open_early(x_peers, to_x)
     open_late(x_peers, to_x)
-    pl.when(c == 1)(lambda: reduce_y(0))
-    second.wait()
+    taken(ld.at[2], obs)
     for i in range(nb):
         a_band(1, i)
+    reduce_y(0)
     local_c(1)
-    pl.when(c == 1)(lambda: reduce_y(1))
-    if Z > 1:
-        z_forward(1)
-    pl.when(c == 0)(lambda: reduce_y(0))
-    if Z > 2:
-        z_forward(2)
     local_b(0)
-    for k in range(3, Z):
-        z_forward(k)
-    pl.when(c == 0)(lambda: reduce_y(1))
-    for i in range(1, nb):
-        local_b(i)
+    reduce_y(1)
+    for k in range(1, max(Z, nb)):
+        if k < Z:
+            from_z(k)
+        if k < nb:
+            local_b(k)
+    reduce_z(0)
     for ky in range(1, Y):
-        y_forward(0, ky)
-    reduce_z(0)
+        from_y(0, ky)
     for k in range(1, nr):
         theirs = rt.at[c, span(rm(k), half)]
-        arrive(theirs, gx_s.at[k - 1], gx_r.at[k - 1])
-        send(theirs, theirs, gp_s.at[k - 1], gp_r.at[k - 1], other)
+        taken(gx.at[k - 1], half)
+        send(0, theirs, theirs, gp.at[0], other)
+    if nr > 1:
+        taken(gp.at[0], (nr - 1) * half)
+    make_g(0, rt)
+    reduce_z(1)
+    make_grad(0, gr_out)
+    rx[r] = finish_z(0).astype(BF16)
+    for k in range(1, nr):
+        send(1, rx.at[r], rx.at[r], xr.at[0], {"region": rp(k)})
     for ky in range(1, Y):
         for k in range(1, Z):
-            y_forward(k, ky)
-    reduce_z(1)
-    for k in range(1, nr):
-        arrive(rt.at[oc, span(rm(k), half)], gp_s.at[k - 1], gp_r.at[k - 1])
-    make_g(0, rt)
-    rx[r] = finish_z(0).astype(BF16)
-    for k in range(1, nr):
-        send(rx.at[r], rx.at[r], xs_s.at[k - 1], xs_r.at[k - 1], {"region": rp(k)})
-    make_grad(0, gr_out)
-    for ky in range(Y):
-        for kz in range(Z):
-            i = ky * Z + kz
-            arrive(block(kz, ky, oc), gc_s.at[i], gc_r.at[i])
+            from_y(k, ky)
+    taken(gc.at[0], K)
     make_g(1, rg)
     make_grad(1, gg_out)
     fg_out[0] = dot(finish_z(1).astype(BF16), g[1])
-    for k in range(1, nr):
-        arrive(rx.at[rm(k)], xs_s.at[k - 1], xs_r.at[k - 1])
+    if nr > 1:
+        taken(xr.at[0], (nr - 1) * rows)
     total = rx[0].astype(F32)
     for k in range(1, nr):
         total += rx[k].astype(F32)
     fr_out[...] = dot(total.astype(BF16), g[0])
-    for copy in sends:
-        copy.wait_send()
+    for kind in range(2):
+        taken(out_sem.at[kind], sent[kind])
 
 
 def store(*refs):
@@ -341,7 +303,6 @@
     def on_device(whiten, leaf_root, leaf_region, root_factor, root_adjoint, region_factor, region_adjoint):
         obs, K = leaf_root.shape[1], leaf_root.shape[2]
         rows = K // nl
-        parts = K // max(min(256, K), 2 * Y * rows)
         dma = lambda n: pltpu.SemaphoreType.DMA((max(n, 1),))
         flag = lambda n: pltpu.SemaphoreType.REGULAR((max(n, 1),))
         args = [pltpu.with_memory_space_constraint(x, pltpu.HBM) for x in (
@@ -371,16 +332,8 @@
                 pltpu.VMEM((2, max(Z - 1, 1), rows, K), BF16),
                 pltpu.VMEM((2, max(Z - 1, 1), rows, K), BF16),
                 pltpu.VMEM((nr, rows, K), BF16),
-                dma(5), pltpu.SemaphoreType.DMA((2, obs // min(256, K))),
-                dma(Z - 1), dma(Z - 1),
-                dma((Y - 1) * Z), dma((Y - 1) * Z),
-                dma(Y * Z), dma(Y * Z),
-                dma(nr - 1), dma(nr - 1),
-                dma(nr - 1), dma(nr - 1),
-                dma(2 * parts), dma(2 * parts),
-                dma(2 * Y * Z), dma(2 * Y * Z),
-                dma(2 * Z), dma(2 * Z),
-                dma(nr - 1), dma(nr - 1),
+                dma(3), dma(obs // min(256, K)), dma(2),
+                dma(Z - 1), dma((Y - 1) * Z), dma(1), dma(nr - 1), dma(1), dma(2), dma(2 * Z), dma(2), dma(1),
                 flag(Z - 1), flag(Y - 1), flag(1), flag(nr - 1),
             ],
             compiler_params=pltpu.CompilerParams(

time: 26.8 us -> 25 us (0.933)
  Pallas kernels: 26 us -> 24.1 us
    pallas_call x1, Pallas kernels: 24.7 us -> 22.7 us  [on_device(): pl.pallas_call(functools.partial(kernel, nr, nl), out_shape=(jax.ShapeDty...]
where the time goes in v3:
time: 25 us; the launch traced here: 24.8 us
  Pallas kernels  24.1 us (96%)
  between operations  0.64 us (3%)
    pallas_call x1, Pallas kernels, on_device(): pl.pallas_call(functools.partial(kernel, nr, nl), out_shape=(jax.ShapeDty...  22.7 us
    pallas_call x1, Pallas kernels, on_device(): pl.pallas_call(store, out_shape=tuple((jax.ShapeDtypeStruct(x.shape, x.dt...  1.38 us

profile of v3, /device:TPU:0, one launch (start us, length us, event | category | flops | bytes accessed | tf_op | source)
XLA Modules:
  0.0 24.8 jit_solution(16355699283862193923)
XLA Ops:
  0.6 22.7 %likelihood_backward.1 = (bf16[1,1024,512]{2,1,0:T(8,128)(2,1)S(1)}, bf16[1,1024,512]{2,1,0:T(8,128)(2,1)S(1)}, f32[32,512]{1,0:T(8,128)S(1)}, f32[1,32,512]{2,1,0:T(8,128)S(1)}) custom-call(bf16[1,1024,1024]{2,1,0:T(8,128)(2,1)} %w_in.1, bf16[1,1024,512]{2,1,0:T(8,128)(2,1)} %lr_in.1, bf16[1,1024,512]{2,1,0:T(8,128)(2,1)} %lg_in.1, bf16[256,512]{1,0:T(8,128)(2,1)} %rf_in.1, ...), custom_call_target="tpu_custom_call" | custom-call | tf_op jit(solution)/shard_map/likelihood_backward/pallas_call | solution.py:310
  23.4 1.4 %store_outputs.1 = (bf16[1,1024,512]{2,1,0:T(8,128)(2,1)}, bf16[1,1024,512]{2,1,0:T(8,128)(2,1)}, f32[32,512]{1,0:T(8,128)}, f32[1,32,512]{2,1,0:T(8,128)}) custom-call(bf16[1,1024,512]{2,1,0:T(8,128)(2,1)S(1)} %get-tuple-element.8.refs_0_, bf16[1,1024,512]{2,1,0:T(8,128)(2,1)S(1)} %get-tuple-element.9.refs_1_, f32[32,512]{1,0:T(8,128)S(1)} %get-tuple-element.10.refs_2_, ...), custom_call_target="tpu_custom_call" | custom-call | tf_op jit(solution)/shard_map/store_outputs/pallas_call | solution.py:344

commit v4 on v3

--- a/solution.py
+++ b/solution.py
@@ -39,7 +39,7 @@
     w_in, lr_in, lg_in, rf_in, ra_in, gf_in, ga_in,
     gr_out, gg_out, fr_out, fg_out,
     w, l, a, b, rt, rg, g, cb, rc, ys, ry, zs, rz, rx,
-    ld, lb, out_sem, gz, gy, gc, gx, gp, cs, yr, zr, xr, zn, yn, cn, xn,
+    ld, lb, out_sem, gz, gf, gy, gc, gx, gp, cs, yr, zr, xr, zn, yn, cn, xn,
 ):
     Z, Y = split_leaf(nl)
     obs, K = l.shape[1], l.shape[2]
@@ -129,39 +129,62 @@
     def block(kz, ky, cc):
         return rg.at[:, span(at(zm(kz), ym(ky), cc), rows)]
 
-    def to_ys(kz):
+    relayed = [k for k in range(3, Z, 2)] if Z & (Z - 1) == 0 else []
+
+    def to_zs(ref, sems):
         return [
-            plan(0, block(kz, 0, c), block(kz, 0, c), gy.at[(k - 1) * Z + kz], {"leaf": at(z, yp(k), c)})
-            for k in range(1, Y)
+            plan(0, ref, ref, sems.at[k - 1], z_peers[k - 1][0]) if k not in relayed else None for k in range(1, Z)
         ]
 
-    def to_core(kz, ky):
-        return plan(0, block(kz, ky, c), block(kz, ky, c), gc.at[0], other)
+    def relay(kz, ref, sems):
+        if kz + 1 in relayed:
+            plan(0, ref, ref, sems.at[kz], z_peers[0][0]).start()
+
+    def to_ys(ref, kz):
+        return [plan(0, ref, ref, gy.at[(k - 1) * Z + kz], y_peers[k - 1][0]) for k in range(1, Y)]
+
+    def to_core(ref):
+        return plan(0, ref, ref, gc.at[0], other)
 
     def from_z(kz):
         taken(gz.at[kz - 1], 2 * rows)
-        for copy in to_ys(kz) + [to_core(kz, 0)]:
+        relay(kz, block(kz, 0, c), gz)
+        for copy in to_ys(block(kz, 0, c).at[1], kz) + [to_core(block(kz, 0, c))]:
             copy.start()
 
+    def from_own_y(ky):
+        taken(gy.at[(ky - 1) * Z], 2 * rows)
+        for copy in to_zs(block(0, ky, c).at[0], gf.at[ky - 1]):
+            if copy:
+                copy.start()
+        to_core(block(0, ky, c)).start()
+
     def from_y(kz, ky):
-        taken(gy.at[(ky - 1) * Z + kz], 2 * rows)
-        to_core(kz, ky).start()
-
-    to_z = [plan(0, block(0, 0, c), block(0, 0, c), gz.at[k - 1], z_peers[k - 1][0]) for k in range(1, Z)]
-    to_y = to_ys(0)
-    to_c = [to_core(0, 0)]
+        taken(gy.at[(ky - 1) * Z + kz], rows)
+        to_core(block(kz, ky, c).at[1]).start()
+
+    def from_y_z(kz, ky):
+        taken(gf.at[ky - 1, kz - 1], rows)
+        relay(kz, block(kz, ky, c).at[0], gf.at[ky - 1])
+        to_core(block(kz, ky, c).at[0]).start()
+
+    to_z = to_zs(block(0, 0, c), gz)
+    to_y = to_ys(block(0, 0, c), 0)
+    to_c = [to_core(block(0, 0, c))]
     to_x = [plan(0, rt.at[c, own], rt.at[c, own], gx.at[k - 1], x_peers[k - 1][0]) for k in range(1, nr)]
 
     def open_early(group, copies):
         for (_, later, _, _), copy in zip(group, copies):
-            pl.when(jnp.logical_not(later))(copy.start)
+            if copy:
+                pl.when(jnp.logical_not(later))(copy.start)
 
     def open_late(group, copies):
         for (_, later, sem, _), copy in zip(group, copies):
             @pl.when(later)
             def _():
                 pl.semaphore_wait(sem, 1)
-                copy.start()
+                if copy:
+                    copy.start()
 
     scale = 1.0 / obs
 
@@ -248,16 +271,22 @@
         a_band(1, i)
     reduce_y(0)
     local_c(1)
+    for ky in range(1, Y):
+        from_own_y(ky)
     local_b(0)
     reduce_y(1)
     for k in range(1, max(Z, nb)):
-        if k < Z:
+        if k < Z and k not in relayed:
             from_z(k)
         if k < nb:
             local_b(k)
     reduce_z(0)
     for ky in range(1, Y):
-        from_y(0, ky)
+        for k in range(1, Z):
+            if k not in relayed:
+                from_y_z(k, ky)
+    for k in relayed:
+        from_z(k)
     for k in range(1, nr):
         theirs = rt.at[c, span(rm(k), half)]
         taken(gx.at[k - 1], half)
@@ -271,6 +300,8 @@
     for k in range(1, nr):
         send(1, rx.at[r], rx.at[r], xr.at[0], {"region": rp(k)})
     for ky in range(1, Y):
+        for k in relayed:
+            from_y_z(k, ky)
         for k in range(1, Z):
             from_y(k, ky)
     taken(gc.at[0], K)
@@ -333,7 +364,7 @@
                 pltpu.VMEM((2, max(Z - 1, 1), rows, K), BF16),
                 pltpu.VMEM((nr, rows, K), BF16),
                 dma(3), dma(obs // min(256, K)), dma(2),
-                dma(Z - 1), dma((Y - 1) * Z), dma(1), dma(nr - 1), dma(1), dma(2), dma(2 * Z), dma(2), dma(1),
+                dma(Z - 1), pltpu.SemaphoreType.DMA((max(Y - 1, 1), max(Z - 1, 1))), dma((Y - 1) * Z), dma(1), dma(nr - 1), dma(1), dma(2), dma(2 * Z), dma(2), dma(1),
                 flag(Z - 1), flag(Y - 1), flag(1), flag(nr - 1),
             ],
             compiler_params=pltpu.CompilerParams(

time: 25 us -> 23.1 us (0.924)
  the two profiles are of different devices: /device:TPU:0 before, /device:TPU:1 now
where the time goes in v4:
time: 23.1 us; the launch traced here: 23 us
  Pallas kernels  22.3 us (97%)
  between operations  0.64 us (3%)
    pallas_call x1, Pallas kernels, on_device(): pl.pallas_call(functools.partial(kernel, nr, nl), out_shape=(jax.ShapeDty...  21 us
    pallas_call x1, Pallas kernels, on_device(): pl.pallas_call(store, out_shape=tuple((jax.ShapeDtypeStruct(x.shape, x.dt...  1.38 us

profile of v4, /device:TPU:1, one launch (start us, length us, event | category | flops | bytes accessed | tf_op | source)
XLA Modules:
  0.0 23.0 jit_solution(17140956797503770632)
XLA Ops:
  0.6 21.0 %likelihood_backward.1 = (bf16[1,1024,512]{2,1,0:T(8,128)(2,1)S(1)}, bf16[1,1024,512]{2,1,0:T(8,128)(2,1)S(1)}, f32[32,512]{1,0:T(8,128)S(1)}, f32[1,32,512]{2,1,0:T(8,128)S(1)}) custom-call(bf16[1,1024,1024]{2,1,0:T(8,128)(2,1)} %w_in.1, bf16[1,1024,512]{2,1,0:T(8,128)(2,1)} %lr_in.1, bf16[1,1024,512]{2,1,0:T(8,128)(2,1)} %lg_in.1, bf16[256,512]{1,0:T(8,128)(2,1)} %rf_in.1, ...), custom_call_target="tpu_custom_call" | custom-call | tf_op jit(solution)/shard_map/likelihood_backward/pallas_call | solution.py:341
  21.6 1.4 %store_outputs.1 = (bf16[1,1024,512]{2,1,0:T(8,128)(2,1)}, bf16[1,1024,512]{2,1,0:T(8,128)(2,1)}, f32[32,512]{1,0:T(8,128)}, f32[1,32,512]{2,1,0:T(8,128)}) custom-call(bf16[1,1024,512]{2,1,0:T(8,128)(2,1)S(1)} %get-tuple-element.8.refs_0_, bf16[1,1024,512]{2,1,0:T(8,128)(2,1)S(1)} %get-tuple-element.9.refs_1_, f32[32,512]{1,0:T(8,128)S(1)} %get-tuple-element.10.refs_2_, ...), custom_call_target="tpu_custom_call" | custom-call | tf_op jit(solution)/shard_map/store_outputs/pallas_call | solution.py:375

commit v5 on v4

--- a/solution.py
+++ b/solution.py
@@ -149,7 +149,8 @@
     def from_z(kz):
         taken(gz.at[kz - 1], 2 * rows)
         relay(kz, block(kz, 0, c), gz)
-        for copy in to_ys(block(kz, 0, c).at[1], kz) + [to_core(block(kz, 0, c))]:
+        held = block(kz, 0, c)
+        for copy in to_ys(held if kz in relayed else held.at[1], kz) + [to_core(held)]:
             copy.start()
 
     def from_own_y(ky):
@@ -160,12 +161,12 @@
         to_core(block(0, ky, c)).start()
 
     def from_y(kz, ky):
-        taken(gy.at[(ky - 1) * Z + kz], rows)
-        to_core(block(kz, ky, c).at[1]).start()
+        held = block(kz, ky, c)
+        taken(gy.at[(ky - 1) * Z + kz], 2 * rows if kz in relayed else rows)
+        to_core(held if kz in relayed else held.at[1]).start()
 
     def from_y_z(kz, ky):
         taken(gf.at[ky - 1, kz - 1], rows)
-        relay(kz, block(kz, ky, c).at[0], gf.at[ky - 1])
         to_core(block(kz, ky, c).at[0]).start()
 
     to_z = to_zs(block(0, 0, c), gz)
@@ -259,12 +260,15 @@
     for i in range(nb):
         taken(lb.at[i], (i + 1) * T * T // K + T)
         a_band(0, i)
+    near = z >= Z // 2
     open_late(c_peers, to_c)
-    open_late(y_peers, to_y)
-    open_late(z_peers, to_z)
-    local_c(0)
     taken(ld.at[1], 2 * half)
     open_early(x_peers, to_x)
+    pl.when(near)(lambda: open_late(y_peers, to_y))
+    pl.when(near)(lambda: open_late(z_peers, to_z))
+    local_c(0)
+    pl.when(jnp.logical_not(near))(lambda: open_late(y_peers, to_y))
+    pl.when(jnp.logical_not(near))(lambda: open_late(z_peers, to_z))
     open_late(x_peers, to_x)
     taken(ld.at[2], obs)
     for i in range(nb):
@@ -285,23 +289,21 @@
         for k in range(1, Z):
             if k not in relayed:
                 from_y_z(k, ky)
-    for k in relayed:
-        from_z(k)
     for k in range(1, nr):
         theirs = rt.at[c, span(rm(k), half)]
         taken(gx.at[k - 1], half)
         send(0, theirs, theirs, gp.at[0], other)
+    for k in relayed:
+        from_z(k)
+    reduce_z(1)
     if nr > 1:
         taken(gp.at[0], (nr - 1) * half)
     make_g(0, rt)
-    reduce_z(1)
     make_grad(0, gr_out)
     rx[r] = finish_z(0).astype(BF16)
     for k in range(1, nr):
         send(1, rx.at[r], rx.at[r], xr.at[0], {"region": rp(k)})
     for ky in range(1, Y):
-        for k in relayed:
-            from_y_z(k, ky)
         for k in range(1, Z):
             from_y(k, ky)
     taken(gc.at[0], K)

time: 23.1 us -> 22.3 us (0.965)
  the two profiles are of different devices: /device:TPU:1 before, /device:TPU:0 now
where the time goes in v5:
time: 22.3 us; the launch traced here: 22.1 us
  Pallas kernels  21.5 us (96%)
  between operations  0.64 us (3%)
    pallas_call x1, Pallas kernels, on_device(): pl.pallas_call(functools.partial(kernel, nr, nl), out_shape=(jax.ShapeDty...  20.1 us
    pallas_call x1, Pallas kernels, on_device(): pl.pallas_call(store, out_shape=tuple((jax.ShapeDtypeStruct(x.shape, x.dt...  1.38 us

profile of v5, /device:TPU:0, one launch (start us, length us, event | category | flops | bytes accessed | tf_op | source)
XLA Modules:
  0.0 22.1 jit_solution(16323024525553591959)
XLA Ops:
  0.6 20.1 %likelihood_backward.1 = (bf16[1,1024,512]{2,1,0:T(8,128)(2,1)S(1)}, bf16[1,1024,512]{2,1,0:T(8,128)(2,1)S(1)}, f32[32,512]{1,0:T(8,128)S(1)}, f32[1,32,512]{2,1,0:T(8,128)S(1)}) custom-call(bf16[1,1024,1024]{2,1,0:T(8,128)(2,1)} %w_in.1, bf16[1,1024,512]{2,1,0:T(8,128)(2,1)} %lr_in.1, bf16[1,1024,512]{2,1,0:T(8,128)(2,1)} %lg_in.1, bf16[256,512]{1,0:T(8,128)(2,1)} %rf_in.1, ...), custom_call_target="tpu_custom_call" | custom-call | tf_op jit(solution)/shard_map/likelihood_backward/pallas_call | solution.py:343
  20.7 1.4 %store_outputs.1 = (bf16[1,1024,512]{2,1,0:T(8,128)(2,1)}, bf16[1,1024,512]{2,1,0:T(8,128)(2,1)}, f32[32,512]{1,0:T(8,128)}, f32[1,32,512]{2,1,0:T(8,128)}) custom-call(bf16[1,1024,512]{2,1,0:T(8,128)(2,1)S(1)} %get-tuple-element.8.refs_0_, bf16[1,1024,512]{2,1,0:T(8,128)(2,1)S(1)} %get-tuple-element.9.refs_1_, f32[32,512]{1,0:T(8,128)S(1)} %get-tuple-element.10.refs_2_, ...), custom_call_target="tpu_custom_call" | custom-call | tf_op jit(solution)/shard_map/store_outputs/pallas_call | solution.py:377

commit v6 on v5

--- a/solution.py
+++ b/solution.py
@@ -231,8 +231,8 @@
             total += ry[p, k - 1, kz].astype(F32)
         return total
 
-    def reduce_z(p):
-        for k in far[:-1]:
+    def reduce_z(p, ks=None):
+        for k in ks or far[:-1]:
             zs[p, k - 1] = chip_sum(p, k).astype(BF16)
             send(1, zs.at[p, k - 1], rz.at[p, k - 1], zr.at[p], {"leaf": at(zp(k), y, c)})
 
@@ -279,12 +279,15 @@
         from_own_y(ky)
     local_b(0)
     reduce_y(1)
+    for k in relayed:
+        from_z(k - 1)
     for k in range(1, max(Z, nb)):
-        if k < Z and k not in relayed:
+        if k < Z and k not in relayed and k + 1 not in relayed:
             from_z(k)
-        if k < nb:
+        if k < nb - 1:
             local_b(k)
     reduce_z(0)
+    local_b(nb - 1)
     for ky in range(1, Y):
         for k in range(1, Z):
             if k not in relayed:
@@ -293,9 +296,10 @@
         theirs = rt.at[c, span(rm(k), half)]
         taken(gx.at[k - 1], half)
         send(0, theirs, theirs, gp.at[0], other)
+    reduce_z(1, far[:1])
     for k in relayed:
         from_z(k)
-    reduce_z(1)
+    reduce_z(1, far[1:-1])
     if nr > 1:
         taken(gp.at[0], (nr - 1) * half)
     make_g(0, rt)

time: 22.3 us -> 22.1 us (level)
  no operation moved by 1% of the time
where the time goes in v6:
time: 22.1 us; the launch traced here: 21.9 us
  Pallas kernels  21.3 us (96%)
  between operations  0.64 us (3%)
    pallas_call x1, Pallas kernels, on_device(): pl.pallas_call(functools.partial(kernel, nr, nl), out_shape=(jax.ShapeDty...  19.9 us
    pallas_call x1, Pallas kernels, on_device(): pl.pallas_call(store, out_shape=tuple((jax.ShapeDtypeStruct(x.shape, x.dt...  1.38 us

profile of v6, /device:TPU:0, one launch (start us, length us, event | category | flops | bytes accessed | tf_op | source)
XLA Modules:
  0.0 21.9 jit_solution(17876505267110421592)
XLA Ops:
  0.6 19.9 %likelihood_backward.1 = (bf16[1,1024,512]{2,1,0:T(8,128)(2,1)S(1)}, bf16[1,1024,512]{2,1,0:T(8,128)(2,1)S(1)}, f32[32,512]{1,0:T(8,128)S(1)}, f32[1,32,512]{2,1,0:T(8,128)S(1)}) custom-call(bf16[1,1024,1024]{2,1,0:T(8,128)(2,1)} %w_in.1, bf16[1,1024,512]{2,1,0:T(8,128)(2,1)} %lr_in.1, bf16[1,1024,512]{2,1,0:T(8,128)(2,1)} %lg_in.1, bf16[256,512]{1,0:T(8,128)(2,1)} %rf_in.1, ...), custom_call_target="tpu_custom_call" | custom-call | tf_op jit(solution)/shard_map/likelihood_backward/pallas_call | solution.py:347
  20.5 1.4 %store_outputs.1 = (bf16[1,1024,512]{2,1,0:T(8,128)(2,1)}, bf16[1,1024,512]{2,1,0:T(8,128)(2,1)}, f32[32,512]{1,0:T(8,128)}, f32[1,32,512]{2,1,0:T(8,128)}) custom-call(bf16[1,1024,512]{2,1,0:T(8,128)(2,1)S(1)} %get-tuple-element.8.refs_0_, bf16[1,1024,512]{2,1,0:T(8,128)(2,1)S(1)} %get-tuple-element.9.refs_1_, f32[32,512]{1,0:T(8,128)S(1)} %get-tuple-element.10.refs_2_, ...), custom_call_target="tpu_custom_call" | custom-call | tf_op jit(solution)/shard_map/store_outputs/pallas_call | solution.py:381

commit v7 on v6

--- a/solution.py
+++ b/solution.py
@@ -287,7 +287,6 @@
         if k < nb - 1:
             local_b(k)
     reduce_z(0)
-    local_b(nb - 1)
     for ky in range(1, Y):
         for k in range(1, Z):
             if k not in relayed:
@@ -297,6 +296,7 @@
         taken(gx.at[k - 1], half)
         send(0, theirs, theirs, gp.at[0], other)
     reduce_z(1, far[:1])
+    local_b(nb - 1)
     for k in relayed:
         from_z(k)
     reduce_z(1, far[1:-1])

time: 22.1 us -> 22.1 us (level)
  no operation moved by 1% of the time
where the time goes in v7:
time: 22.1 us; the launch traced here: 21.9 us
  Pallas kernels  21.3 us (96%)
  between operations  0.64 us (3%)
    pallas_call x1, Pallas kernels, on_device(): pl.pallas_call(functools.partial(kernel, nr, nl), out_shape=(jax.ShapeDty...  19.9 us
    pallas_call x1, Pallas kernels, on_device(): pl.pallas_call(store, out_shape=tuple((jax.ShapeDtypeStruct(x.shape, x.dt...  1.38 us

profile of v7, /device:TPU:0, one launch (start us, length us, event | category | flops | bytes accessed | tf_op | source)
XLA Modules:
  0.0 21.9 jit_solution(601536929356875720)
XLA Ops:
  0.6 19.9 %likelihood_backward.1 = (bf16[1,1024,512]{2,1,0:T(8,128)(2,1)S(1)}, bf16[1,1024,512]{2,1,0:T(8,128)(2,1)S(1)}, f32[32,512]{1,0:T(8,128)S(1)}, f32[1,32,512]{2,1,0:T(8,128)S(1)}) custom-call(bf16[1,1024,1024]{2,1,0:T(8,128)(2,1)} %w_in.1, bf16[1,1024,512]{2,1,0:T(8,128)(2,1)} %lr_in.1, bf16[1,1024,512]{2,1,0:T(8,128)(2,1)} %lg_in.1, bf16[256,512]{1,0:T(8,128)(2,1)} %rf_in.1, ...), custom_call_target="tpu_custom_call" | custom-call | tf_op jit(solution)/shard_map/likelihood_backward/pallas_call | solution.py:347
  20.5 1.4 %store_outputs.1 = (bf16[1,1024,512]{2,1,0:T(8,128)(2,1)}, bf16[1,1024,512]{2,1,0:T(8,128)(2,1)}, f32[32,512]{1,0:T(8,128)}, f32[1,32,512]{2,1,0:T(8,128)}) custom-call(bf16[1,1024,512]{2,1,0:T(8,128)(2,1)S(1)} %get-tuple-element.8.refs_0_, bf16[1,1024,512]{2,1,0:T(8,128)(2,1)S(1)} %get-tuple-element.9.refs_1_, f32[32,512]{1,0:T(8,128)S(1)} %get-tuple-element.10.refs_2_, ...), custom_call_target="tpu_custom_call" | custom-call | tf_op jit(solution)/shard_map/store_outputs/pallas_call | solution.py:381
